TPU v7x, 8 devices: a whole 2x2x1 slice. The times are simulated.
8 devices in a mesh: tp: 2 (over z, y), fsdp: 4 (over x, core).
Axes of the slice: x: 2, y: 2, z: 1, core: 2. Of those that a mesh axis runs over, the one named last changes fastest.
Arguments:
- resid_in: bfloat16 [8, 6144, 3584], P('fsdp', 'tp')
- grad_out: bfloat16 [8, 6144, 3584], P('fsdp', 'tp')
- norm_gain: float32 [3584], replicated
- w_qkv: bfloat16 [3584, 4608], P('fsdp', 'tp')
- b_qkv: bfloat16 [4608], P('tp')
- sinks: float32 [28], P('tp')
- w_out: bfloat16 [3584, 3584], P(('tp', 'fsdp'))
- b_out: bfloat16 [3584], replicated
Outputs:
- output 1: bfloat16 [8, 6144, 3584], P('fsdp', 'tp')
- output 2: bfloat16 [8, 6144, 3584], P('fsdp', 'tp')
- output 3: float32 [3584], replicated
- output 4: float32 [3584, 4608], P('fsdp', 'tp')
- output 5: float32 [4608], P('tp')
- output 6: float32 [28], P('tp')
- output 7: float32 [3584, 3584], P(('tp', 'fsdp'))
- output 8: float32 [3584], replicated
All inputs are finite; a program needn't handle non-finite values.
Results may differ from a plain program's by a relative error of at most 0.0114246.
Values are sent between devices in bfloat16 or wider.
A program may use at most 1 GiB of HBM per device.

v0:
```python
import jax
import jax.numpy as jnp
from jax import lax
from jax.sharding import PartitionSpec as P

EPS = 1e-5
ROPE_BASE = 150000.0
WINDOW = 128


def rope_tables(positions, head_dim):
    inv_freq = ROPE_BASE ** (-2.0 * jnp.arange(head_dim // 2).astype(jnp.float32) / head_dim)
    angles = positions.astype(jnp.float32)[:, None] * inv_freq[None, :]
    return jnp.cos(angles), jnp.sin(angles)


def apply_rope(head_vals, cos_tab, sin_tab):
    half_dim = head_vals.shape[-1] // 2
    first_half = head_vals[..., :half_dim]
    second_half = head_vals[..., half_dim:]
    return jnp.concatenate([first_half * cos_tab - second_half * sin_tab, second_half * cos_tab + first_half * sin_tab], axis=-1)


def rope_back(head_grads, cos_tab, sin_tab):
    half_dim = head_grads.shape[-1] // 2
    first_half = head_grads[..., :half_dim]
    second_half = head_grads[..., half_dim:]
    return jnp.concatenate([first_half * cos_tab + second_half * sin_tab, second_half * cos_tab - first_half * sin_tab], axis=-1)


def split_qkv(qkv_proj, positions, kv_count, head_dim):
    n_rows, seq_len = qkv_proj.shape[0], qkv_proj.shape[1]
    grouped = qkv_proj.reshape(n_rows, seq_len, kv_count, -1, head_dim)
    group_size = grouped.shape[3] - 2
    cos_tab, sin_tab = rope_tables(positions, head_dim)
    queries = apply_rope(grouped[:, :, :, :group_size].astype(jnp.float32), cos_tab[:, None, None], sin_tab[:, None, None])
    keys_rot = apply_rope(grouped[:, :, :, group_size].astype(jnp.float32), cos_tab[:, None], sin_tab[:, None])
    return queries.astype(jnp.bfloat16), keys_rot.astype(jnp.bfloat16), grouped[:, :, :, group_size + 1]


def band_mask(first_pos, blk_start):
    q_idx = jnp.arange(WINDOW)[:, None]
    k_idx = jnp.arange(2 * WINDOW)[None, :]
    return (k_idx > q_idx) & (k_idx <= q_idx + WINDOW) & (first_pos + blk_start - WINDOW + k_idx >= 0)


def block_scores(q_blk, k_blk, first_pos, blk_start):
    qk_scale = q_blk.shape[-1] ** -0.5
    scores = jnp.einsum("niegd,njed->negij", q_blk, k_blk, preferred_element_type=jnp.float32) * qk_scale
    return jnp.where(band_mask(first_pos, blk_start), scores, -1e30)


def attend_forward(queries, keys_ext, values_ext, sink_loc, first_pos):
    n_rows, q_len, kv_loc, group_size, head_dim = queries.shape
    sink_col = sink_loc.reshape(1, kv_loc, group_size, 1)

    def block_body(block_idx, loop_carry):
        out_acc, norm_acc = loop_carry
        blk_start = block_idx * WINDOW
        q_blk = lax.dynamic_slice_in_dim(queries, blk_start, WINDOW, axis=1)
        k_blk = lax.dynamic_slice_in_dim(keys_ext, blk_start, 2 * WINDOW, axis=1)
        v_blk = lax.dynamic_slice_in_dim(values_ext, blk_start, 2 * WINDOW, axis=1)
        scores = block_scores(q_blk, k_blk, first_pos, blk_start)
        row_max = jnp.maximum(jnp.max(scores, axis=-1), sink_col)
        exp_scores = jnp.exp(scores - row_max[..., None])
        row_denom = jnp.sum(exp_scores, axis=-1) + jnp.exp(sink_col - row_max)
        attn_probs = (exp_scores / row_denom[..., None]).astype(jnp.bfloat16)
        out_blk = jnp.einsum("negij,njed->niegd", attn_probs, v_blk, preferred_element_type=jnp.float32)
        out_acc = lax.dynamic_update_slice_in_dim(out_acc, out_blk.astype(jnp.bfloat16), blk_start, axis=1)
        norm_acc = lax.dynamic_update_slice_in_dim(norm_acc, row_max + jnp.log(row_denom), blk_start, axis=3)
        return out_acc, norm_acc

    init_carry = (jnp.zeros(queries.shape, jnp.bfloat16), jnp.zeros((n_rows, kv_loc, group_size, q_len), jnp.float32))
    return lax.fori_loop(0, q_len // WINDOW, block_body, init_carry)


def attend_backward(queries, keys_ext, values_ext, sink_loc, first_pos, log_norm, d_out):
    n_rows, q_len, kv_loc, group_size, head_dim = queries.shape
    qk_scale = head_dim ** -0.5
    sink_col = sink_loc.reshape(1, kv_loc, group_size, 1)

    def block_body(block_idx, loop_carry):
        dq_acc, dk_acc, dv_acc, dsink_acc = loop_carry
        blk_start = block_idx * WINDOW
        q_blk = lax.dynamic_slice_in_dim(queries, blk_start, WINDOW, axis=1)
        k_blk = lax.dynamic_slice_in_dim(keys_ext, blk_start, 2 * WINDOW, axis=1)
        v_blk = lax.dynamic_slice_in_dim(values_ext, blk_start, 2 * WINDOW, axis=1)
        do_blk = lax.dynamic_slice_in_dim(d_out, blk_start, WINDOW, axis=1)
        norm_blk = lax.dynamic_slice_in_dim(log_norm, blk_start, WINDOW, axis=3)
        attn_probs = jnp.exp(block_scores(q_blk, k_blk, first_pos, blk_start) - norm_blk[..., None])
        dv_blk = jnp.einsum("negij,niegd->njed", attn_probs.astype(jnp.bfloat16), do_blk, preferred_element_type=jnp.float32)
        d_probs = jnp.einsum("niegd,njed->negij", do_blk, v_blk, preferred_element_type=jnp.float32).astype(jnp.bfloat16).astype(jnp.float32)
        row_dot = jnp.sum(attn_probs * d_probs, axis=-1)
        d_scores = (attn_probs * (d_probs - row_dot[..., None])).astype(jnp.bfloat16)
        sink_probs = jnp.exp(sink_col - norm_blk)
        dsink_acc = dsink_acc - jnp.sum(sink_probs * row_dot, axis=(0, 3))
        dq_blk = jnp.einsum("negij,njed->niegd", d_scores, k_blk, preferred_element_type=jnp.float32) * qk_scale
        dk_blk = jnp.einsum("negij,niegd->njed", d_scores, q_blk, preferred_element_type=jnp.float32) * qk_scale
        dq_acc = lax.dynamic_update_slice_in_dim(dq_acc, dq_blk.astype(jnp.bfloat16), blk_start, axis=1)
        dk_acc = lax.dynamic_update_slice_in_dim(dk_acc, lax.dynamic_slice_in_dim(dk_acc, blk_start, 2 * WINDOW, axis=1) + dk_blk, blk_start, axis=1)
        dv_acc = lax.dynamic_update_slice_in_dim(dv_acc, lax.dynamic_slice_in_dim(dv_acc, blk_start, 2 * WINDOW, axis=1) + dv_blk, blk_start, axis=1)
        return dq_acc, dk_acc, dv_acc, dsink_acc

    init_carry = (jnp.zeros(queries.shape, jnp.bfloat16), jnp.zeros(keys_ext.shape, jnp.float32), jnp.zeros(values_ext.shape, jnp.float32), jnp.zeros((kv_loc, group_size), jnp.float32))
    dq_all, dk_all, dv_all, dsink_all = lax.fori_loop(0, q_len // WINDOW, block_body, init_carry)
    return dq_all, dk_all, dv_all, dsink_all.reshape(-1)


def norm_backward(d_normed, resid_f32, inv_rms, norm_gain, grad_loc):
    d_normed = d_normed.astype(jnp.bfloat16).astype(jnp.float32)
    gain_grad = d_normed * norm_gain
    d_resid = inv_rms * (gain_grad - resid_f32 * inv_rms * inv_rms * jnp.mean(gain_grad * resid_f32, axis=-1, keepdims=True))
    grad_resid = (grad_loc.astype(jnp.float32) + d_resid).astype(jnp.bfloat16)
    grad_gain = jnp.sum(d_normed * resid_f32 * inv_rms, axis=(0, 1))
    return grad_resid, grad_gain


def solution(mesh):
    act_spec = P("fsdp", "tp", None)
    wout_spec = P(("tp", "fsdp"), None)
    in_specs = (act_spec, act_spec, P(), P("fsdp", "tp"), P("tp"), P("tp"), wout_spec, P())
    out_specs = (act_spec, act_spec, P(), P("fsdp", "tp"), P("tp"), P("tp"), wout_spec, P())

    def device_step(resid_loc, grad_loc, norm_gain, wqkv_loc, bqkv_loc, sink_loc, wout_loc, b_out):
        n_rows = resid_loc.shape[0]
        heads_loc = sink_loc.shape[0]
        resid_f32 = resid_loc.astype(jnp.float32)
        inv_rms = lax.rsqrt(jnp.mean(resid_f32 * resid_f32, axis=-1, keepdims=True) + EPS)
        normed = (resid_f32 * inv_rms * norm_gain).astype(jnp.bfloat16)

        wqkv_full = lax.all_gather(wqkv_loc, "fsdp", axis=0, tiled=True)
        wout_full = lax.all_gather(wout_loc, "fsdp", axis=0, tiled=True)
        normed_all = lax.all_gather(normed, "tp", axis=1, tiled=True)
        seq_len = normed_all.shape[1]
        head_dim = wout_full.shape[0] // heads_loc
        kv_loc = (wqkv_full.shape[1] // head_dim - heads_loc) // 2

        qkv_proj = (jnp.dot(normed_all, wqkv_full, preferred_element_type=jnp.float32) + bqkv_loc.astype(jnp.float32)).astype(jnp.bfloat16)
        positions = jnp.arange(seq_len)
        queries, keys_rot, values = split_qkv(qkv_proj, positions, kv_loc, head_dim)
        pad_zeros = jnp.zeros((n_rows, WINDOW, kv_loc, head_dim), jnp.bfloat16)
        keys_ext = jnp.concatenate([pad_zeros, keys_rot], axis=1)
        values_ext = jnp.concatenate([pad_zeros, values], axis=1)
        attn_out, log_norm = attend_forward(queries, keys_ext, values_ext, sink_loc, 0)
        attn_flat = attn_out.reshape(n_rows, seq_len, heads_loc * head_dim)
        part_sum = jnp.dot(attn_flat, wout_full, preferred_element_type=jnp.float32)
        proj_out = lax.psum_scatter(part_sum, "tp", scatter_dimension=1, tiled=True)
        resid_out = (resid_f32 + proj_out + b_out.astype(jnp.float32)).astype(jnp.bfloat16)

        grad_bout = lax.psum(jnp.sum(grad_loc, axis=(0, 1), dtype=jnp.float32), ("fsdp", "tp"))
        grad_all = lax.all_gather(grad_loc, "tp", axis=1, tiled=True)
        wout_part = jnp.einsum("nth,ntk->hk", attn_flat, grad_all, preferred_element_type=jnp.float32)
        grad_wout = lax.psum_scatter(wout_part, "fsdp", scatter_dimension=0, tiled=True)
        d_attn = jnp.einsum("ntk,hk->nth", grad_all, wout_full, preferred_element_type=jnp.float32).astype(jnp.bfloat16)
        dq_rot, dk_ext, dv_ext, sink_part = attend_backward(queries, keys_ext, values_ext, sink_loc, 0, log_norm, d_attn.reshape(attn_out.shape))
        cos_tab, sin_tab = rope_tables(positions, head_dim)
        d_query = rope_back(dq_rot.astype(jnp.float32), cos_tab[:, None, None], sin_tab[:, None, None]).astype(jnp.bfloat16)
        d_key = rope_back(dk_ext[:, WINDOW:].astype(jnp.bfloat16).astype(jnp.float32), cos_tab[:, None], sin_tab[:, None]).astype(jnp.bfloat16)
        d_value = dv_ext[:, WINDOW:].astype(jnp.bfloat16)
        d_qkv = jnp.concatenate([d_query, d_key[:, :, :, None], d_value[:, :, :, None]], axis=3).reshape(qkv_proj.shape)
        wqkv_part = jnp.einsum("ntd,ntc->dc", normed_all, d_qkv, preferred_element_type=jnp.float32)
        grad_wqkv = lax.psum_scatter(wqkv_part, "fsdp", scatter_dimension=0, tiled=True)
        grad_bqkv = lax.psum(jnp.sum(d_qkv, axis=(0, 1), dtype=jnp.float32), "fsdp")
        grad_sinks = lax.psum(sink_part, "fsdp")
        normed_part = jnp.einsum("ntc,dc->ntd", d_qkv, wqkv_full, preferred_element_type=jnp.float32)
        d_normed = lax.psum_scatter(normed_part, "tp", scatter_dimension=1, tiled=True)
        grad_resid, gain_part = norm_backward(d_normed, resid_f32, inv_rms, norm_gain, grad_loc)
        grad_gain = lax.psum(gain_part, ("fsdp", "tp"))
        return (resid_out, grad_resid, grad_gain, grad_wqkv, grad_bqkv, grad_sinks, grad_wout, grad_bout)

    return jax.shard_map(device_step, mesh=mesh, in_specs=in_specs, out_specs=out_specs, check_vma=False)
```

profile of v0, /device:TPU:0, one launch (start us, length us, event | category | flops | bytes accessed | tf_op | source)
XLA Modules:
  0.0 7758.9 jit_solution(6335309480505558898)
XLA Ops:
  13.7 14.7 fusion.64
  28.4 30.2 fusion.60
  67.7 51.5 all-gather.7.cloned.1.call-done
  119.2 1004.5 %all-gather.5.cloned.1.call-done = bf16[2,6144,3584]{2,1,0:T(8,128)(2,1)} async-done(((bf16[2,3072,3584]{2,1,0:T(8,128)(2,1)}), bf16[2,6144,3584]{2,1,0:T(8,128)(2,1)}) %all-gather.5.cloned.1.call-update) | async-done | bytes 88080400 | tf_op jit(solution)/shard_map/all_gather | solution.py:133
  1123.6 218.0 %add_convert_fusion = bf16[2,6144,2304]{1,2,0:T(8,128)(2,1)} fusion(bf16[2,6144,3584]{2,1,0:T(8,128)(2,1)} %all-gather.5.cloned.1.call-done, f32[2304]{0:T(1024)S(1)} %convert_element_type.224, bf16[3584,2304]{0,1:T(8,128)(2,1)} %all-gather.7.cloned.1.call-done), kind=kOutput, calls=%fused_computation.80 | convolution fusion | flops 202993827840 | bytes 161227776 | tf_op jit(solution)/shard_map/dot_general | solution.py:138
  1341.6 11.9 fusion.78
  1353.5 44.1 slice_convert_fusion
  1415.3 43.2 subtract_convert_fusion.1
  1458.5 29.6 pad_maximum_fusion.1
  1488.1 52.0 copy.47
  1552.2 14.3 broadcast.284.clone
  1566.5 294.3 %while.39 = (s32[]{:T(128)}, bf16[2,6144,2,7,128]{1,4,3,2,0:T(8,128)(2,1)}, f32[2,2,7,6144]{3,2,1,0:T(8,128)S(1)}, bf16[2,6272,2,128]{1,3,2,0:T(8,128)(2,1)}, bf...) while((s32[]{:T(128)}, ...), condition=%wide.region_4.5_spmd, body=%wide.region_1.4_spmd.sunk | while | flops 481373312 | bytes 13669152 | solution.py:74
  1860.8 349.6 %all-gather.11.cloned.1.call-done = bf16[2,6144,3584]{2,1,0:T(8,128)(2,1)} async-done(((bf16[2,3072,3584]{2,1,0:T(8,128)(2,1)}), bf16[2,6144,3584]{2,1,0:T(8,128)(2,1)}) %all-gather.11.cloned.1.call-update) | async-done | bytes 88080400 | tf_op jit(solution)/shard_map/all_gather | solution.py:151
  2210.4 171.3 %convolution_convert_fusion.1 = bf16[2,6144,1792]{1,2,0:T(8,128)(2,1)} fusion(bf16[2,6144,3584]{2,1,0:T(8,128)(2,1)} %all-gather.11.cloned.1.call-done, bf16[1792,3584]{1,0:T(8,128)(2,1)} %all-gather.9.cloned.1.call-done), kind=kOutput, calls=%fused_computation.104 | convolution fusion | flops 157862068224 | bytes 144965632 | tf_op jit(solution)/shard_map/ntk,hk->nth/dot_general | solution.py:154
  2392.5 14.3 broadcast.284
  2406.8 780.2 %while.40 = (s32[]{:T(128)}, bf16[2,6144,2,7,128]{1,4,3,2,0:T(8,128)(2,1)}, f32[2,6272,2,128]{1,3,2,0:T(8,128)}, f32[2,6272,2,128]{1,3,2,0:T(8,128)}, f32[2,7]{1...) while((s32[]{:T(128)}, ...), condition=%wide.region_9.10_spmd.clone, body=%wide.region_6.9_spmd.clone.sunk | while | flops 1186864768 | bytes 29659212 | solution.py:105
  3195.4 10.6 fusion.76
  3213.2 43.0 convert_element_type.235
  3256.1 42.7 add_convert_fusion.1
  3298.9 39.0 convert_reduce_fusion
  3337.8 220.2 %fusion.70 = f32[2,6144,3584]{2,1,0:T(8,128)} fusion(bf16[2,6144,2304]{1,2,0:T(8,128)(2,1)} %bitcast.182, bf16[3584,2304]{0,1:T(8,128)(2,1)} %all-gather.7.cloned.1.call-done), kind=kOutput, calls=%fused_computation.107 | convolution fusion | flops 202937204736 | bytes 249298944 | tf_op jit(solution)/shard_map/ntc,dc->ntd/dot_general | solution.py:165
  3558.2 175.5 %fusion.74 = f32[2,6144,3584]{2,1,0:T(8,128)} fusion(bf16[2,6144,1792]{1,2,0:T(8,128)(2,1)} %bitcast.184, bf16[1792,3584]{1,0:T(8,128)(2,1)} %all-gather.9.cloned.1.call-done), kind=kOutput, calls=%fused_computation.111 | convolution fusion | flops 157840048128 | bytes 233046016 | tf_op jit(solution)/shard_map/dot_general | solution.py:146
  3733.8 194.3 %convolution_bitcast_fusion.2 = f32[1792,3584]{1,0:T(8,128)} fusion(bf16[2,6144,1792]{1,2,0:T(8,128)(2,1)} %bitcast.185, bf16[2,6144,3584]{2,1,0:T(8,128)(2,1)} %all-gather.11.cloned.1.call-done), kind=kOutput, calls=%fused_computation.106 | convolution fusion | flops 157840048128 | bytes 157810688 | tf_op jit(solution)/shard_map/nth,ntk->hk/dot_general | solution.py:152
  3928.1 221.2 %convolution_bitcast_fusion.1 = f32[3584,2304]{1,0:T(8,128)} fusion(bf16[2,6144,3584]{2,1,0:T(8,128)(2,1)} %all-gather.5.cloned.1.call-done, bf16[2,6144,2304]{1,2,0:T(8,128)(2,1)} %bitcast.183), kind=kOutput, calls=%fused_computation.105 | convolution fusion | flops 202937204736 | bytes 177733632 | tf_op jit(solution)/shard_map/ntd,ntc->dc/dot_general | solution.py:161
  4150.7 12.3 all-reduce.3
  4163.0 1289.5 %reduce-scatter.7.cloned.1.call-done = f32[2,3072,3584]{2,1,0:T(8,128)} async-done(((f32[2,6144,3584]{2,1,0:T(8,128)}), f32[2,3072,3584]{2,1,0:T(8,128)}) %reduce-scatter.7.cloned.1.call-update) | async-done | bytes 88080400 | tf_op jit(solution)/shard_map/reduce_scatter | solution.py:166
  5452.5 41.2 fusion.69
  5493.8 1855.2 %reduce-scatter.5.cloned.1.call-done = f32[2,3072,3584]{2,1,0:T(8,128)} async-done(((f32[2,6144,3584]{2,1,0:T(8,128)}), f32[2,3072,3584]{2,1,0:T(8,128)}) %reduce-scatter.5.cloned.1.call-update) | async-done | bytes 88080400 | tf_op jit(solution)/shard_map/reduce_scatter | solution.py:147
  7349.0 110.5 %convert_reduce_fusion.1 = (f32[3584]{0:T(1024)S(1)}, bf16[2,3072,3584]{2,1,0:T(8,128)(2,1)}, bf16[2,3072,3584]{2,1,0:T(8,128)(2,1)}) fusion(bf16[2,3072,3584]{2,1,0:T(8,128)(2,1)} %param.13, f32[2,3072]{1,0:T(2,128)S(1)} %broadcast_multiply_fusion, bf16[2,3072,3584]{2,1,0:T(8,128)(2,1)} %param.12, f32[3584]{0:T(1024)S(1)} %copy-done.10, ...), kind=kLoop, calls=%fused_computation.82 | loop fusion | flops 352317952 | bytes 352413696 | tf_op jit(solution)/shard_map/reduce_sum | solution.py:150
  7459.4 23.6 all-reduce.2
  7483.0 42.7 reduce-scatter.11.cloned.1.call-done
  7525.7 226.1 %reduce-scatter.9.cloned.1.call-done = f32[896,2304]{1,0:T(8,128)} async-done(((f32[3584,2304]{1,0:T(8,128)}), f32[896,2304]{1,0:T(8,128)}) %reduce-scatter.9.cloned.1.call-update) | async-done | bytes 8257552 | tf_op jit(solution)/shard_map/reduce_scatter | solution.py:162
  (1029 shorter events, 1145.3 us)
Async XLA Ops:
  7.2 112.0 %all-gather.7.cloned.1.call-start = ((), (), s32[]{:S(2)}) async-start(), calls=%async_computation.5 | async-start | bytes 20643840 | tf_op jit(solution)/shard_map/all_gather | solution.py:131
  13.6 14.8 copy-start.9
  13.6 1110.0 %all-gather.5.cloned.1.call-start = ((), (), s32[]{:S(2)}) async-start(), calls=%async_computation.4 | async-start | bytes 132120576 | tf_op jit(solution)/shard_map/all_gather | solution.py:133
  28.4 30.2 copy-start.5
  58.7 1802.1 %all-gather.9.cloned.1.call-start = ((), (), s32[]{:S(2)}) async-start(), calls=%async_computation.6 | async-start | bytes 16056320 | tf_op jit(solution)/shard_map/all_gather | solution.py:132
  59.4 0.7 copy-start.14
  59.4 1.3 copy-start.13
  59.4 2150.9 %all-gather.11.cloned.1.call-start = ((), (), s32[]{:S(2)}) async-start(), calls=%async_computation.8 | async-start | bytes 132120576 | tf_op jit(solution)/shard_map/all_gather | solution.py:151
  60.0 5392.5 %reduce-scatter.7.cloned.1.call-start = ((), (), s32[]{:S(2)}) async-start(), calls=%async_computation.9 | async-start | bytes 264241152 | tf_op jit(solution)/shard_map/reduce_scatter | solution.py:166
  1353.5 44.1 copy-start
  1353.5 44.1 copy-start.2
  1552.2 14.3 copy-start.7
  1860.8 520.9 %copy-start.4 = (f32[2,2,7,6144]{3,2,1,0:T(8,128)}, f32[2,2,7,6144]{3,2,1,0:T(8,128)S(1)}, u32[]{:S(2)}) copy-start(f32[2,2,7,6144]{3,2,1,0:T(8,128)S(1)} %get-tuple-element.763) | copy-start | bytes 2064388
  2392.5 14.3 copy-start.8
  3187.0 18.9 copy-start.1
  3187.1 18.9 copy-start.3
  3558.1 3790.9 %reduce-scatter.5.cloned.1.call-start = ((), (), s32[]{:S(2)}) async-start(), calls=%async_computation.7 | async-start | bytes 264241152 | tf_op jit(solution)/shard_map/reduce_scatter | solution.py:147
  3733.7 3792.0 %reduce-scatter.11.cloned.1.call-start = ((), (), s32[]{:S(2)}) async-start(), calls=%async_computation.11 | async-start | bytes 32112640 | tf_op jit(solution)/shard_map/reduce_scatter | solution.py:153
  3928.1 3823.8 %reduce-scatter.9.cloned.1.call-start = ((), (), s32[]{:S(2)}) async-start(), calls=%async_computation.10 | async-start | bytes 41287680 | tf_op jit(solution)/shard_map/reduce_scatter | solution.py:162
  4149.3 0.7 copy-start.12
  4149.3 1.5 copy-start.11
  4149.3 1303.3 %copy-start.6 = (f32[2,3072]{1,0:T(2,128)S(1)}, f32[2,3072]{1,0:T(2,128)}, u32[]{:S(2)}) copy-start(f32[2,3072]{1,0:T(2,128)} %copy-done.5) | copy-start | bytes 73732
  4149.3 1303.3 %copy-start.10 = (f32[3584]{0:T(1024)S(1)}, f32[3584]{0:T(1024)}, u32[]{:S(2)}) copy-start(f32[3584]{0:T(1024)} %param.14) | copy-start | bytes 43012
Sparse Core Ops, SparseCore 0:
  13.7 105.3 all-gather.6
  121.3 1002.2 all-gather.4
  1125.1 81.4 all-gather.8
  1208.0 1002.2 all-gather.10
  3558.2 1894.2 reduce-scatter.6
  5454.7 1894.2 reduce-scatter.4
  7352.1 173.5 reduce-scatter.10
  7528.9 222.9 reduce-scatter.8
where the time goes:
time: 7790 us; the launch traced here: 7760 us
  waiting for transfers between devices  4820 us (62%)
  matrix products  2050 us (26%)
  other arithmetic  674 us (9%)
  local copies, waits for them, and re-layouts  164 us (2%)
    reduce_scatter x1, waiting for transfers between devices, device_step(): proj_out = lax.psum_scatter(part_sum, 'tp', scatter_dimension=1, tiled=True)  1860 us
    reduce_scatter x1, waiting for transfers between devices, device_step(): lax.psum_scatter(normed_part, 'tp', scatter_dimension=1, tiled=True)  1290 us
    all_gather x1, waiting for transfers between devices, device_step(): normed_all = lax.all_gather(normed, 'tp', axis=1, tiled=True)  1000 us
    all_gather x1, waiting for transfers between devices, device_step(): grad_all = lax.all_gather(grad_loc, 'tp', axis=1, tiled=True)  350 us
    reduce_scatter x1, waiting for transfers between devices, device_step(): lax.psum_scatter(wqkv_part, 'fsdp', scatter_dimension=0, tiled=True)  226 us
    dot_general x1, matrix products, device_step(): jnp.einsum('ntd,ntc->dc', normed_all, d_qkv, preferred_element_type=jnp.f...  221 us
    dot_general x1, matrix products, device_step(): jnp.einsum('ntc,dc->ntd', d_qkv, wqkv_full, preferred_element_type=jnp.fl...  220 us
    dot_general x1, matrix products, device_step(): jnp.dot(normed_all, wqkv_full, preferred_element_type=jnp.float32)  218 us
  transfers between devices with their start and end apart: 8, of which 7 were waited for; matrix products, arithmetic and copies ran while one was open for 20% of the time, Pallas kernels for 0%

commit v1 on v0

v1 whole, which is shorter than its diff:
```python
import functools

import jax
import jax.numpy as jnp
from jax import lax
from jax.experimental import pallas as pl
from jax.experimental.pallas import tpu as pltpu
from jax.sharding import PartitionSpec as P

EPS = 1e-5
ROPE_BASE = 150000.0
W = 128
HD = 128
GROUP = 7
COLS = (GROUP + 2) * HD
QCOLS = GROUP * HD
SCALE = HD ** -0.5
LOG2E = 1.4426950408889634
NEG = -1e30
F32 = jnp.float32
BF16 = jnp.bfloat16
NT = (((1,), (1,)), ((), ()))
NN = (((1,), (0,)), ((), ()))
HEAD_SETS = ((0, 1), (2, 3), (4, 5, 6))
VMEM_LIMIT = 66_000_000


def rope_tables(positions, head_dim):
    inv_freq = ROPE_BASE ** (-2.0 * jnp.arange(head_dim // 2).astype(F32) / head_dim)
    angles = positions.astype(F32)[:, None] * inv_freq[None, :]
    return jnp.cos(angles), jnp.sin(angles)


def rope_back(head_grads, cos_tab, sin_tab):
    half_dim = head_grads.shape[-1] // 2
    first_half = head_grads[..., :half_dim]
    second_half = head_grads[..., half_dim:]
    return jnp.concatenate([first_half * cos_tab + second_half * sin_tab, second_half * cos_tab - first_half * sin_tab], axis=-1)


def dot(a, b, dims):
    return lax.dot_general(a, b, dims, preferred_element_type=F32)


def attn_body(n_blocks, flags, sinks, qkv, d_attn, halo, cos2, sin2, cos_t, sin_t, upper_bf, _, attn, d_qkv, dkv_halo, dkv_last, col_sum, d_sink, k_cat, v_cat, k_t, v_t, dk_acc, dv_acc):
    group = pl.program_id(1)
    has_prev = flags[0] > 0
    row = lax.broadcasted_iota(jnp.int32, (W, W), 0)
    col = lax.broadcasted_iota(jnp.int32, (W, W), 1)
    upper = row > col

    k_halo = halo[0, 0, :, :HD].astype(F32)
    k_halo = (k_halo * cos2[:W, :] + pltpu.roll(k_halo, HD // 2, 1) * sin2[:W, :]).astype(BF16)
    k_cat[W:, :] = k_halo
    v_cat[W:, :] = halo[0, 0, :, HD:]
    k_t[:, W:] = k_halo.T
    v_t[:, W:] = halo[0, 0, :, HD:].T
    dk_acc[...] = jnp.zeros_like(dk_acc)
    dv_acc[...] = jnp.zeros_like(dv_acc)
    col_sum[...] = jnp.zeros_like(col_sum)
    d_sink[...] = jnp.zeros_like(d_sink)

    def block(b, first):
        r0 = 0 if first else pl.multiple_of(b * W, W)
        rows = pl.ds(r0, W)
        tab_rows = pl.ds(r0 + W, W)
        cos_b, sin_b = cos2[tab_rows, :], sin2[tab_rows, :]
        cos_c, sin_c = cos_t[:, rows], sin_t[:, rows]

        def rotate(raw):
            wide = raw.astype(F32)
            return (wide * cos_b + pltpu.roll(wide, HD // 2, 1) * sin_b).astype(BF16)

        k_new = rotate(qkv[rows, QCOLS:QCOLS + HD])
        v_new = qkv[rows, QCOLS + HD:]
        k_cat[:W, :] = k_cat[W:, :]
        v_cat[:W, :] = v_cat[W:, :]
        k_t[:, :W] = k_t[:, W:]
        v_t[:, :W] = v_t[:, W:]
        k_cat[W:, :] = k_new
        v_cat[W:, :] = v_new
        k_t[:, W:] = k_new.T
        v_t[:, W:] = v_new.T
        keys, values = k_cat[...], v_cat[...]
        keys_t, values_t = k_t[...], v_t[...]
        mask_bf = upper_bf[...]

        dk, dv = [], []

        def ahead(heads):
            q_set = jnp.concatenate([rotate(qkv[rows, h * HD:(h + 1) * HD]) for h in heads], axis=0)
            do_set = jnp.concatenate([d_attn[rows, h * HD:(h + 1) * HD] for h in heads], axis=0)
            return q_set, do_set, dot(keys, q_set, NT), dot(values, do_set, NT)

        def softmax(heads, q_set, do_set, scores, d_prob2):
            probs, d_scores = [], []
            for i, h in enumerate(heads):
                lanes = slice(i * W, (i + 1) * W)
                s_prev = scores[:W, lanes]
                if first:
                    s_prev = jnp.where(has_prev, s_prev, NEG)
                s = jnp.where(upper, s_prev, scores[W:, lanes])
                s = s * (SCALE * LOG2E)
                sink = sinks[group * GROUP + h] * LOG2E
                top = jnp.maximum(jnp.max(s, axis=0, keepdims=True), sink)
                e = jnp.exp2(s - top)
                e_sink = jnp.exp2(sink - top)
                inv = 1.0 / (jnp.sum(e, axis=0, keepdims=True) + e_sink)
                p = e * inv
                dp = jnp.where(upper, d_prob2[:W, lanes], d_prob2[W:, lanes]).astype(BF16).astype(F32)
                row_dot = jnp.sum(p * dp, axis=0, keepdims=True)
                d_sink[0, 0, h:h + 1, :] -= (e_sink * inv) * row_dot
                p_bf = p.astype(BF16)
                ds_bf = (p * (dp - row_dot)).astype(BF16)
                p_prev = p_bf * mask_bf
                ds_prev = ds_bf * mask_bf
                probs.append(jnp.concatenate([p_prev, p_bf - p_prev], axis=0))
                d_scores.append(jnp.concatenate([ds_prev, ds_bf - ds_prev], axis=0))
            return q_set, do_set, jnp.concatenate(probs, axis=1), jnp.concatenate(d_scores, axis=1)

        def behind(heads, q_set, do_set, p_set, ds_set):
            dv.append(dot(p_set, do_set, NN))
            dk.append(dot(ds_set, q_set, NN))
            return dot(values_t, p_set, NN), dot(keys_t, ds_set, NN)

        def store(heads, out_t, dq_t):
            for i, h in enumerate(heads):
                lanes = slice(i * W, (i + 1) * W)
                cols = slice(h * HD, (h + 1) * HD)
                attn[rows, cols] = out_t[:, lanes].astype(BF16).T
                g = (dq_t[:, lanes] * SCALE).astype(BF16).astype(F32)
                g1, g2 = g[:HD // 2], g[HD // 2:]
                dq = jnp.concatenate([g1 * cos_c + g2 * sin_c, g2 * cos_c - g1 * sin_c], axis=0).astype(BF16).T
                d_qkv[rows, cols] = dq
                col_sum[0, 0, 0:1, cols] += jnp.sum(dq.astype(F32), axis=0, keepdims=True)

        stages = (ahead, softmax, behind, store)
        held = [()] * len(HEAD_SETS)
        for tick in range(len(HEAD_SETS) + len(stages) - 1):
            for k in range(len(stages)):
                i = tick - k
                if 0 <= i < len(HEAD_SETS):
                    held[i] = stages[k](HEAD_SETS[i], *held[i])
        dk, dv = sum(dk[1:], dk[0]), sum(dv[1:], dv[0])

        if first:
            dkv_halo[0, 0, :, :HD] = dk[:W]
            dkv_halo[0, 0, :, HD:] = dv[:W]
        else:
            done = pl.ds(pl.multiple_of(b * W - W, W), W)
            g = ((dk_acc[...] + dk[:W]) * SCALE).astype(BF16).astype(F32)
            dk_out = (g * cos2[rows, :] - pltpu.roll(g, HD // 2, 1) * sin2[rows, :]).astype(BF16)
            dv_out = (dv_acc[...] + dv[:W]).astype(BF16)
            d_qkv[done, QCOLS:QCOLS + HD] = dk_out
            d_qkv[done, QCOLS + HD:] = dv_out
            col_sum[0, 0, 0:1, QCOLS:QCOLS + HD] += jnp.sum(dk_out.astype(F32), axis=0, keepdims=True)
            col_sum[0, 0, 0:1, QCOLS + HD:] += jnp.sum(dv_out.astype(F32), axis=0, keepdims=True)
        dk_acc[...] = dk[W:]
        dv_acc[...] = dv[W:]

    block(0, True)

    def step(b, carry):
        block(b, False)
        return carry

    lax.fori_loop(1, n_blocks, step, 0)
    dkv_last[0, 0, :, :HD] = dk_acc[...]
    dkv_last[0, 0, :, HD:] = dv_acc[...]
    last = pl.ds((n_blocks - 1) * W, W)
    d_qkv[last, QCOLS:] = jnp.zeros((W, 2 * HD), BF16)


def attention(piece, flags, sinks, qkv, d_attn, halo, cos2, sin2, attn_buf, n_rows, seq):
    tokens = n_rows * seq
    groups = qkv.shape[1] // COLS
    upper_bf = (jnp.arange(W)[:, None] > jnp.arange(W)[None, :]).astype(BF16)
    cos_t, sin_t = cos2[W:, :HD // 2].T, sin2[W:, HD // 2:].T
    once = pl.Buffered(1)
    const = lambda *shape: pl.BlockSpec(shape, lambda n, e: (0,) * len(shape), pipeline_mode=once)
    part = lambda *shape: pl.BlockSpec((1, 1) + shape, lambda n, e: (n, e) + (0,) * len(shape))
    wide = pl.BlockSpec((seq, COLS), lambda n, e: (n, e))
    heads = pl.BlockSpec((seq, QCOLS), lambda n, e: (n, piece * groups + e))
    out_shape = (
        jax.ShapeDtypeStruct((tokens, d_attn.shape[1]), BF16),
        jax.ShapeDtypeStruct((tokens, qkv.shape[1]), BF16),
        jax.ShapeDtypeStruct((n_rows, groups, W, 2 * HD), F32),
        jax.ShapeDtypeStruct((n_rows, groups, W, 2 * HD), F32),
        jax.ShapeDtypeStruct((n_rows, groups, 8, COLS), F32),
        jax.ShapeDtypeStruct((n_rows, groups, 8, W), F32),
    )
    any_spec = pl.BlockSpec(memory_space=pl.ANY)
    smem = pl.BlockSpec(memory_space=pltpu.SMEM)
    in_specs = [smem, smem, wide, heads, part(W, 2 * HD), const(seq + W, HD), const(seq + W, HD), const(HD // 2, seq), const(HD // 2, seq), const(W, W), any_spec]
    operands = [flags, sinks, qkv, d_attn, halo, cos2, sin2, cos_t, sin_t, upper_bf, attn_buf]
    aliases = {10: 0}
    if attn_buf is None:
        operands[10] = jnp.zeros((8, 128), BF16)
        aliases = {}
    pair_macs = tokens * groups * GROUP * 2 * W * HD
    return pl.pallas_call(
        functools.partial(attn_body, seq // W),
        name=f"attention_{piece}",
        grid=(n_rows, groups),
        in_specs=in_specs,
        out_specs=(heads, wide, part(W, 2 * HD), part(W, 2 * HD), part(8, COLS), part(8, W)),
        out_shape=out_shape,
        scratch_shapes=[pltpu.VMEM((2 * W, HD), BF16)] * 2 + [pltpu.VMEM((HD, 2 * W), BF16)] * 2 + [pltpu.VMEM((W, HD), F32)] * 2,
        input_output_aliases=aliases,
        compiler_params=pltpu.CompilerParams(vmem_limit_bytes=VMEM_LIMIT),
        cost_estimate=pl.CostEstimate(flops=24 * pair_macs, bytes_accessed=8 * tokens * groups * COLS, transcendentals=tokens * groups * GROUP * W),
    )(*operands)


def norm_forward_body(x, gain, out):
    wide = x[...].astype(F32)
    inv = lax.rsqrt(jnp.mean(wide * wide, axis=-1, keepdims=True) + EPS)
    out[...] = (wide * inv * gain[0:1, :]).astype(BF16)


def norm_forward(x, gain):
    tokens, width = x.shape
    tile = min(512, tokens)
    block = pl.BlockSpec((tile, width), lambda i: (i, 0))
    return pl.pallas_call(
        norm_forward_body,
        name="norm_forward",
        grid=(tokens // tile,),
        in_specs=[block, pl.BlockSpec((8, width), lambda i: (0, 0))],
        out_specs=block,
        out_shape=jax.ShapeDtypeStruct(x.shape, BF16),
        compiler_params=pltpu.CompilerParams(vmem_limit_bytes=VMEM_LIMIT),
        cost_estimate=pl.CostEstimate(flops=4 * tokens * width, bytes_accessed=4 * tokens * width, transcendentals=tokens),
    )(x, jnp.broadcast_to(gain[None, :], (8, width)))


def norm_backward_body(dh, x, dy, gain, dx, sums):
    @pl.when(pl.program_id(0) == 0)
    def _():
        sums[...] = jnp.zeros_like(sums)

    wide = x[...].astype(F32)
    grad = dh[...].astype(F32)
    up = dy[...].astype(F32)
    inv = lax.rsqrt(jnp.mean(wide * wide, axis=-1, keepdims=True) + EPS)
    gain_grad = grad * gain[0:1, :]
    proj = jnp.mean(gain_grad * wide, axis=-1, keepdims=True)
    dx[...] = (up + inv * (gain_grad - wide * (inv * inv * proj))).astype(BF16)
    sums[0:1, :] += jnp.sum(grad * wide * inv, axis=0, keepdims=True)
    sums[1:2, :] += jnp.sum(up, axis=0, keepdims=True)


def norm_backward(dh, x, dy, gain):
    tokens, width = x.shape
    tile = min(256, tokens)
    block = pl.BlockSpec((tile, width), lambda i: (i, 0))
    small = pl.BlockSpec((8, width), lambda i: (0, 0))
    return pl.pallas_call(
        norm_backward_body,
        name="norm_backward",
        grid=(tokens // tile,),
        in_specs=[block, block, block, small],
        out_specs=(block, small),
        out_shape=(jax.ShapeDtypeStruct(x.shape, BF16), jax.ShapeDtypeStruct((8, width), F32)),
        compiler_params=pltpu.CompilerParams(vmem_limit_bytes=VMEM_LIMIT),
        cost_estimate=pl.CostEstimate(flops=12 * tokens * width, bytes_accessed=8 * tokens * width, transcendentals=tokens),
    )(dh, x, dy, jnp.broadcast_to(gain[None, :], (8, width)))


def unwritten(shape, dtype):
    return pl.pallas_call(
        lambda out: None,
        name="unwritten",
        out_specs=pl.BlockSpec(memory_space=pl.ANY),
        out_shape=jax.ShapeDtypeStruct(shape, dtype),
    )()


def solution(mesh):
    act_spec = P("fsdp", "tp", None)
    wout_spec = P(("tp", "fsdp"), None)
    in_specs = (act_spec, act_spec, P(), P("fsdp", "tp"), P("tp"), P("tp"), wout_spec, P())
    out_specs = (act_spec, act_spec, P(), P("fsdp", "tp"), P("tp"), P("tp"), wout_spec, P())
    both = ("tp", "fsdp")
    n_tp = mesh.shape["tp"]

    def device_step(resid_loc, grad_loc, norm_gain, wqkv_loc, bqkv_loc, sink_loc, wout_loc, b_out):
        n_rows, seq, width = resid_loc.shape
        tokens = n_rows * seq
        here = lax.axis_index("tp")
        x = resid_loc.reshape(tokens, width)
        dy = grad_loc.reshape(tokens, width)
        groups = wqkv_loc.shape[1] // COLS
        heads_loc = sink_loc.shape[0]

        wout = lax.all_gather(wout_loc, both, axis=0, tiled=True)
        normed = norm_forward(x, norm_gain)
        wqkv_loc, normed = lax.optimization_barrier((wqkv_loc, normed))
        wqkv = lax.all_gather(wqkv_loc, both, axis=0, tiled=True).reshape(n_tp, width, -1)
        bqkv = lax.all_gather(bqkv_loc, "tp", axis=0, tiled=True).reshape(n_tp, -1).astype(F32)
        sinks = lax.all_gather(sink_loc, "tp", axis=0, tiled=True)

        d_attn = dot(dy, wout, NT).astype(BF16)
        normed, d_attn = lax.optimization_barrier((normed, d_attn))
        cos_tab, sin_tab = rope_tables(here * seq - W + jnp.arange(seq + W), HD)
        cos2 = jnp.concatenate([cos_tab, cos_tab], axis=1)
        sin2 = jnp.concatenate([-sin_tab, sin_tab], axis=1)
        flags = here.astype(jnp.int32).reshape(1)

        qkv = [(dot(normed, wqkv[t], NN) + bqkv[t]).astype(BF16) for t in range(n_tp)]
        halos = []
        for t in range(n_tp):
            tails = [[qkv[t][(n + 1) * seq - W:(n + 1) * seq, e * COLS + QCOLS:(e + 1) * COLS] for e in range(groups)] for n in range(n_rows)]
            halos.append(lax.ppermute(jnp.stack([jnp.stack(row) for row in tails]), "tp", [(i, i + 1) for i in range(n_tp - 1)]))

        attn, d_qkv, col_sums, d_sinks = None, [], [], []
        for t in range(n_tp):
            attn, dq, dkv_halo, dkv_last, col_sum, d_sink = attention(t, flags, sinks[t * heads_loc:(t + 1) * heads_loc], qkv[t], d_attn, halos[t], cos2, sin2, attn, n_rows, seq)
            dkv = dkv_last + lax.ppermute(dkv_halo, "tp", [(i + 1, i) for i in range(n_tp - 1)])
            dk = (dkv[..., :HD] * SCALE).astype(BF16).astype(F32)
            dk = rope_back(dk, cos_tab[seq:], sin_tab[seq:]).astype(BF16)
            dkv = jnp.concatenate([dk, dkv[..., HD:].astype(BF16)], axis=-1)
            for n in range(n_rows):
                for e in range(groups):
                    dq = lax.dynamic_update_slice(dq, dkv[n, e], (n * seq + seq - W, e * COLS + QCOLS))
            d_qkv.append(dq)
            total = jnp.sum(col_sum[:, :, 0], axis=0)
            col_sums.append(total.at[:, QCOLS:].add(jnp.sum(dkv, axis=(0, 2), dtype=F32)).reshape(-1))
            d_sinks.append(jnp.sum(d_sink[:, :, :GROUP], axis=(0, 3)).reshape(-1))

        over_tokens = (((0,), (0,)), ((), ()))
        grad_wout = lax.psum_scatter(dot(attn, dy, over_tokens), both, scatter_dimension=0, tiled=True)
        wqkv_part = unwritten((n_tp * width, wqkv.shape[2]), F32)
        for t in range(n_tp):
            wqkv_part = lax.dynamic_update_slice(wqkv_part, dot(normed, d_qkv[t], over_tokens), (t * width, 0))
        grad_wqkv = lax.psum_scatter(wqkv_part, both, scatter_dimension=0, tiled=True)

        d_normed = dot(d_qkv[0], wqkv[0], NT)
        for t in range(1, n_tp):
            d_normed = d_normed + dot(d_qkv[t], wqkv[t], NT)
        grad_resid, sums = norm_backward(d_normed.astype(BF16), x, dy, norm_gain)

        resid_out = (x.astype(F32) + dot(attn, wout, NN) + b_out.astype(F32)).astype(BF16)

        small = lax.psum(jnp.concatenate([sums[0], sums[1]] + col_sums + d_sinks), both)
        n_cols = groups * COLS
        grad_gain, grad_bout = small[:width], small[width:2 * width]
        grad_bqkv = lax.dynamic_slice(small, (2 * width + here * n_cols,), (n_cols,))
        grad_sinks = lax.dynamic_slice(small, (2 * width + n_tp * n_cols + here * heads_loc,), (heads_loc,))
        return (resid_out.reshape(resid_loc.shape), grad_resid.reshape(resid_loc.shape), grad_gain, grad_wqkv, grad_bqkv, grad_sinks, grad_wout, grad_bout)

    return jax.shard_map(device_step, mesh=mesh, in_specs=in_specs, out_specs=out_specs, check_vma=False)
```

time: 7790 us -> 1750 us (0.22)
  waiting for transfers between devices: 4820 us -> 84.6 us
  matrix products: 2050 us -> 1210 us
  other arithmetic: 674 us -> 11.2 us
  Pallas kernels: 0 us -> 350 us
  local copies, waits for them, and re-layouts: 164 us -> 26.3 us
    reduce_scatter x4 -> x2, waiting for transfers between devices: 3410 us -> 0.01 us  [the longest x1 0.01 us: device_step(): lax.psum_scatter(dot(attn, dy, over_tokens), both, scatter_dimension=0, t...]
    all_gather x4 -> x2, waiting for transfers between devices: 1410 us -> 61.4 us  [the longest x1 61.3 us: device_step(): wout = lax.all_gather(wout_loc, both, axis=0, tiled=True)]
    dot_general x342 -> x9, matrix products: 2050 us -> 1210 us  [dot(): return lax.dot_general(a, b, dims, preferred_element_type=F32)]
    pallas_call x0 -> x5, Pallas kernels: none -> 350 us  [the longest x2 226 us: attention(): pl.pallas_call(functools.partial(attn_body, seq // W), name=f'attention_{...]
    reduce_sum x100 -> x6, other arithmetic: 287 us -> 4.66 us  [the longest x2 3.09 us: device_step(): total = jnp.sum(col_sum[:, :, 0], axis=0)]
    convert_element_type x56 -> x6, other arithmetic: 171 us -> 0.71 us  [the longest x1 0.63 us: attention(): upper_bf = (jnp.arange(W)[:, None] > jnp.arange(W)[None, :]).astype(BF16)]
    another operation x3 -> x5, other arithmetic: 91.5 us -> 1.07 us  [the longest x4 0.81 us: device_step(): jnp.stack([jnp.stack(row) for row in tails])]
  transfers between devices with their start and end apart: 8 -> 8, of which waited for: 7 -> 3; matrix products, arithmetic and copies ran while one was open for 20% -> 55% of each run, Pallas kernels for 0% -> 14%
where the time goes in v1:
time: 1750 us; the launch traced here: 1740 us
  matrix products  1210 us (69%)
  Pallas kernels  350 us (20%)
  waiting for transfers between devices  84.6 us (5%)
  blocking collectives  33.5 us (2%)
  local copies, waits for them, and re-layouts  26.3 us (2%)
    dot_general x9, matrix products, dot(): return lax.dot_general(a, b, dims, preferred_element_type=F32)  1210 us
    pallas_call x2, Pallas kernels, attention(): pl.pallas_call(functools.partial(attn_body, seq // W), name=f'attention_{...  226 us
    pallas_call x1, Pallas kernels, norm_backward(): pl.pallas_call(norm_backward_body, name='norm_backward', grid=(tokens //...  84.9 us
    all_gather x1, waiting for transfers between devices, device_step(): wout = lax.all_gather(wout_loc, both, axis=0, tiled=True)  61.3 us
    pallas_call x1, Pallas kernels, norm_forward(): pl.pallas_call(norm_forward_body, name='norm_forward', grid=(tokens // ti...  39.5 us
  transfers between devices with their start and end apart: 8, of which 3 were waited for; matrix products, arithmetic and copies ran while one was open for 55% of the time, Pallas kernels for 14%

profile of v1, /device:TPU:0, one launch (start us, length us, event | category | flops | bytes accessed | tf_op | source)
XLA Modules:
  0.0 1741.2 jit_solution(17391545573595652205)
XLA Ops:
  7.9 1.4 broadcast_in_dim.4.gain
  9.3 39.5 %norm_forward.1 = bf16[6144,3584]{1,0:T(8,128)(2,1)} custom-call(bf16[6144,3584]{1,0:T(8,128)(2,1)} %bitcast.84, f32[8,3584]{1,0:T(8,128)} %broadcast_in_dim.4.gain), custom_call_target="tpu_custom_call" | custom-call | flops 88080384 | bytes 88080384 | tf_op jit(solution)/shard_map/norm_forward/pallas_call | solution.py:225
  48.9 5.9 all-gather
  54.9 2.9 fusion.7
  57.8 1.6 pad_maximum_fusion
  59.5 2.7 copy.25.cos2
  62.1 1.7 copy.26.sin2
  65.3 5.0 all-reduce
  72.2 1.3 slice_bitcast_fusion
  73.5 61.3 %all-gather.4.cloned.1.call-done = bf16[3584,3584]{1,0:T(8,128)(2,1)} async-done(((bf16[448,3584]{1,0:T(8,128)(2,1)}), bf16[3584,3584]{1,0:T(8,128)(2,1)}) %all-gather.4.cloned.1.call-update) | async-done | bytes 25690128 | tf_op jit(solution)/shard_map/all_gather | solution.py:296
  134.8 175.9 %convolution_convert_fusion.d_attn = bf16[6144,3584]{1,0:T(8,128)(2,1)} fusion(bf16[6144,3584]{1,0:T(8,128)(2,1)} %bitcast.87, bf16[3584,3584]{1,0:T(8,128)(2,1)} %all-gather.4.cloned.1.call-done), kind=kOutput, calls=%fused_computation.4 | convolution fusion | flops 157862068224 | bytes 113770496 | tf_op jit(solution)/shard_map/dot_general | solution.py:42
  310.8 113.6 %add_convert_fusion.2.qkv = bf16[6144,2304]{1,0:T(8,128)(2,1)} fusion(bf16[6144,3584]{1,0:T(8,128)(2,1)} %norm_forward.1, f32[2304]{0:T(1024)S(1)} %copy-done.11, bf16[7168,2304]{1,0:T(8,128)(2,1)} %all-gather.6.cloned.1.call-done), kind=kOutput, calls=%fused_computation.2 | convolution fusion | flops 101496913920 | bytes 88876032 | tf_op jit(solution)/shard_map/dot_general | solution.py:42
  426.1 2.9 collective-permute-start.1
  429.1 113.8 %add_convert_fusion.3.qkv = bf16[6144,2304]{1,0:T(8,128)(2,1)} fusion(bf16[6144,3584]{1,0:T(8,128)(2,1)} %norm_forward.1, f32[2304]{0:T(1024)S(1)} %copy-done.10, bf16[7168,2304]{1,0:T(8,128)(2,1)} %all-gather.6.cloned.1.call-done), kind=kOutput, calls=%fused_computation.3 | convolution fusion | flops 101496913920 | bytes 88876032 | tf_op jit(solution)/shard_map/dot_general | solution.py:42
  543.9 1.3 collective-permute-start
  545.8 112.9 %attention_0.1 = (bf16[6144,3584]{1,0:T(8,128)(2,1)}, bf16[6144,2304]{1,0:T(8,128)(2,1)}, f32[2,2,128,256]{3,2,1,0:T(8,128)}, f32[2,2,128,256]{3,2,1,0:T(8,128)}...) custom-call(s32[1]{0:T(128)} %bitcast.1.flags, f32[14]{0:T(128)} %get-tuple-element.95.sinks, ...), custom_call_target="tpu_custom_call" | custom-call | flops 67645734912 | bytes 113246208 | tf_op jit(solution)/shard_map/attention_0/pallas_call | solution.py:201
  659.4 113.1 %attention_1.1 = (bf16[6144,3584]{1,0:T(8,128)(2,1)}, bf16[6144,2304]{1,0:T(8,128)(2,1)}, f32[2,2,128,256]{3,2,1,0:T(8,128)}, f32[2,2,128,256]{3,2,1,0:T(8,128)}...) custom-call(s32[1]{0:T(128)} %bitcast.1.flags, ...), custom_call_target="tpu_custom_call", output_to_operand_aliasing={{0}: (10, {})} | custom-call | flops 67645734912 | bytes 113246208 | tf_op jit(solution)/shard_map/attention_1/pallas_call | solution.py:201
  772.5 173.7 %fusion.23 = f32[3584,3584]{1,0:T(8,128)} fusion(bf16[6144,3584]{1,0:T(8,128)(2,1)} %get-tuple-element.55, bf16[6144,3584]{1,0:T(8,128)(2,1)} %bitcast.88), kind=kOutput, calls=%fused_computation.83 | convolution fusion | flops 157840048128 | bytes 139460608 | tf_op jit(solution)/shard_map/dot_general | solution.py:42
  947.3 1.3 collective-permute-start.3
  948.6 1.3 collective-permute-start.2
  951.6 12.4 collective-permute-done.3
  964.1 10.1 collective-permute-done.2
  981.2 118.8 %convolution_dynamic-update-slice_fusion.1 = f32[7168,2304]{1,0:T(8,128)} fusion(f32[7168,2304]{1,0:T(8,128)} %unwritten.1, bf16[6144,3584]{1,0:T(8,128)(2,1)} %norm_forward.1, bf16[6144,2304]{1,0:T(8,128)(2,1)} %fusion.14), kind=kOutput, calls=%fused_computation.6 | convolution fusion | flops 101468602368 | bytes 105381888 | tf_op jit(solution)/shard_map/dot_general | solution.py:42
  1100.0 118.7 %convolution_dynamic-update-slice_fusion = f32[7168,2304]{1,0:T(8,128)} fusion(f32[7168,2304]{1,0:T(8,128)} %convolution_dynamic-update-slice_fusion.1, bf16[6144,3584]{1,0:T(8,128)(2,1)} %norm_forward.1, bf16[6144,2304]{1,0:T(8,128)(2,1)} %fusion.10), kind=kOutput, calls=%fused_computation.5 | convolution fusion | flops 101468602368 | bytes 105381888 | tf_op jit(solution)/shard_map/dot_general | solution.py:42
  1220.8 1.5 slice_reduce_fusion
  1222.3 1.5 slice_reduce_fusion.1
  1223.9 171.1 %add_convert_fusion.1 = bf16[6144,3584]{1,0:T(8,128)(2,1)} fusion(bf16[6144,3584]{1,0:T(8,128)(2,1)} %bitcast.85, bf16[6144,3584]{1,0:T(8,128)(2,1)} %get-tuple-element.55, bf16[3584,3584]{1,0:T(8,128)(2,1)} %all-gather.4.cloned.1.call-done, f32[3584]{0:T(1024)S(1)} %convert_element_type.75), kind=kOutput, calls=%fused_computation.1 | convolution fusion | flops 157928128512 | bytes 157825024 | tf_op jit(solution)/shard_map/dot_general | solution.py:42
  1396.2 112.5 %fusion = f32[6144,3584]{1,0:T(8,128)} fusion(bf16[6144,2304]{1,0:T(8,128)(2,1)} %fusion.14, bf16[7168,2304]{1,0:T(8,128)(2,1)} %all-gather.6.cloned.1.call-done), kind=kOutput, calls=%fused_computation.7 | convolution fusion | flops 101468602368 | bytes 132907008 | tf_op jit(solution)/shard_map/dot_general | solution.py:42
  1508.7 115.0 %add_convert_fusion.dh = bf16[6144,3584]{1,0:T(8,128)(2,1)} fusion(f32[6144,3584]{1,0:T(8,128)} %fusion, bf16[6144,2304]{1,0:T(8,128)(2,1)} %fusion.10, bf16[7168,2304]{1,0:T(8,128)(2,1)} %all-gather.6.cloned.1.call-done), kind=kOutput, calls=%fused_computation | convolution fusion | flops 101512642560 | bytes 176947200 | tf_op jit(solution)/shard_map/dot_general | solution.py:42
  1623.7 84.9 %norm_backward.1 = (bf16[6144,3584]{1,0:T(8,128)(2,1)}, f32[8,3584]{1,0:T(8,128)}) custom-call(bf16[6144,3584]{1,0:T(8,128)(2,1)} %add_convert_fusion.dh, bf16[6144,3584]{1,0:T(8,128)(2,1)} %bitcast.86, bf16[6144,3584]{1,0:T(8,128)(2,1)} %bitcast.89, f32[8,3584]{1,0:T(8,128)} %broadcast_in_dim.4.gain), custom_call_target="tpu_custom_call" | custom-call | flops 264241152 | bytes 176160768 | tf_op jit(solution)/shard_map/norm_backward/pallas_call | solution.py:258
  1708.6 1.0 slice_reduce_fusion.4
  1709.8 22.6 %psum.7 = f32[11804]{0:T(1024)S(1)} all-reduce(f32[11804]{0:T(1024)S(1)} %concatenate.29), channel_id=1, replica_groups=mesh['tp'=2,'fsdp'=4] {'tp','fsdp'}, use_global_device_ids=true, to_apply=%region_6.0 | all-reduce | flops 11804 | bytes 94432 | tf_op jit(solution)/shard_map/psum | solution.py:345
  (111 shorter events, 22.7 us)
Async XLA Ops:
  7.2 127.7 %all-gather.4.cloned.1.call-start = ((), (), s32[]{:S(2)}) async-start(), calls=%async_computation.2 | async-start | bytes 28901376 | tf_op jit(solution)/shard_map/all_gather | solution.py:296
  7.9 302.9 %all-gather.6.cloned.1.call-start = ((), (), s32[]{:S(2)}) async-start(), calls=%async_computation.3 | async-start | bytes 37158912 | tf_op jit(solution)/shard_map/all_gather | solution.py:299
  9.3 39.6 %copy-start.15 = (bf16[2304]{0:T(1024)(128)(2,1)S(1)}, bf16[2304]{0:T(1024)(128)(2,1)}, u32[]{:S(2)}) copy-start(bf16[2304]{0:T(1024)(128)(2,1)} %param.16) | copy-start | bytes 13828
  9.3 54.5 %copy-start.22 = (u32[8]{0:T(128)S(1)}, u32[8]{0:T(128)}, u32[]{:S(2)}) copy-start(u32[8]{0:T(128)} %constant.101) | copy-start | bytes 100
  9.3 55.7 %copy-start.21 = (f32[14]{0:T(128)S(1)}, f32[14]{0:T(128)}, u32[]{:S(2)}) copy-start(f32[14]{0:T(128)} %param.17) | copy-start | bytes 172
  48.8 1685.4 %reduce-scatter.5.cloned.1.call-start = ((), (), s32[]{:S(2)}) async-start(), calls=%async_computation.5 | async-start | bytes 57802752 | tf_op jit(solution)/shard_map/reduce_scatter | solution.py:332
  57.8 252.9 %copy-start = (f32[3200,64]{0,1:T(8,128)}, f32[3200,64]{0,1:T(8,128)S(1)}, u32[]{:S(2)}) copy-start(f32[3200,64]{0,1:T(8,128)S(1)} %get-tuple-element.94) | copy-start | bytes 2457604
  57.8 252.9 %copy-start.1 = (f32[3200,64]{0,1:T(8,128)}, f32[3200,64]{0,1:T(8,128)S(1)}, u32[]{:S(2)}) copy-start(f32[3200,64]{0,1:T(8,128)S(1)} %get-tuple-element.93) | copy-start | bytes 2457604
  134.8 175.9 %copy-start.11 = (f32[2304]{0:T(1024)S(1)}, f32[2304]{0:T(1024)}, u32[]{:S(2)}) copy-start(f32[2304]{0:T(1024)} %get-tuple-element.70) | copy-start | bytes 27652
  310.8 118.3 %copy-start.10 = (f32[2304]{0:T(1024)S(1)}, f32[2304]{0:T(1024)}, u32[]{:S(2)}) copy-start(f32[2304]{0:T(1024)} %get-tuple-element.71) | copy-start | bytes 27652
  426.1 119.1 %collective-permute-start.1 = (bf16[2,2,128,256]{3,2,1,0:T(8,128)(2,1)}, bf16[2,2,128,256]{3,2,1,0:T(8,128)(2,1)}, u32[]{:S(2)}, u32[]{:S(2)}) collective-permute-start(bf16[2,2,128,256]{3,2,1,0:T(8,128)(2,1)} %pad_maximum_fusion.3), channel_id=1, source_target_pairs={{0,4},{1,5},{2,6},{3,7}} | collective-permute-start | bytes 786440 | tf_op jit(solution)/shard_map/ppermute | solution.py:314
  543.9 114.9 %collective-permute-start = (bf16[2,2,128,256]{3,2,1,0:T(8,128)(2,1)S(1)}, bf16[2,2,128,256]{3,2,1,0:T(8,128)(2,1)S(1)}, u32[]{:S(2)}, u32[]{:S(2)}) collective-permute-start(bf16[2,2,128,256]{3,2,1,0:T(8,128)(2,1)S(1)} %pad_maximum_fusion.2), channel_id=1, source_target_pairs={{0,4},{1,5},{2,6},{3,7}} | collective-permute-start | bytes 786440 | tf_op jit(solution)/shard_map/ppermute | solution.py:314
  658.7 0.7 copy-start.20
  946.2 1.0 copy-start.19
  946.2 2.3 copy-start.18
  946.3 788.0 %reduce-scatter.3.cloned.1.call-start = ((), (), s32[]{:S(2)}) async-start(), calls=%async_computation.4 | async-start | bytes 74317824 | tf_op jit(solution)/shard_map/reduce_scatter | solution.py:336
  947.3 16.7 collective-permute-start.3
  948.6 25.6 %collective-permute-start.2 = (f32[2,2,128,256]{3,2,1,0:T(8,128)S(1)}, f32[2,2,128,256]{3,2,1,0:T(8,128)S(1)}, u32[]{:S(2)}, u32[]{:S(2)}) collective-permute-start(f32[2,2,128,256]{3,2,1,0:T(8,128)S(1)} %copy-done.18), channel_id=1, source_target_pairs={{4,0},{5,1},{6,2},{7,3}} | collective-permute-start | bytes 1572872 | tf_op jit(solution)/shard_map/ppermute | solution.py:319
  951.4 12.6 copy-start.3
  951.4 22.8 %copy-start.2 = (f32[2,2,128,256]{3,2,1,0:T(8,128)S(1)}, f32[2,2,128,256]{3,2,1,0:T(8,128)}, u32[]{:S(2)}) copy-start(f32[2,2,128,256]{3,2,1,0:T(8,128)} %get-tuple-element.57) | copy-start | bytes 1572868
  1218.7 0.7 copy-start.14
  1218.7 0.7 copy-start.9
  1218.7 1.4 copy-start.8
  1223.9 171.1 %copy-start.7 = (f32[2,1152]{1,0:T(2,128)S(1)}, f32[2,1152]{1,0:T(2,128)}, u32[]{:S(2)}) copy-start(f32[2,1152]{1,0:T(2,128)} %slice_reduce_fusion) | copy-start | bytes 27652
  1223.9 171.1 %copy-start.12 = (f32[2,256]{1,0:T(2,128)S(1)}, f32[2,256]{1,0:T(2,128)}, u32[]{:S(2)}) copy-start(f32[2,256]{1,0:T(2,128)} %get-tuple-element.72) | copy-start | bytes 6148
  1223.9 171.7 %copy-start.6 = (f32[2,1152]{1,0:T(2,128)S(1)}, f32[2,1152]{1,0:T(2,128)}, u32[]{:S(2)}) copy-start(f32[2,1152]{1,0:T(2,128)} %slice_reduce_fusion.1) | copy-start | bytes 27652
  1223.9 171.7 %copy-start.13 = (f32[2,256]{1,0:T(2,128)S(1)}, f32[2,256]{1,0:T(2,128)}, u32[]{:S(2)}) copy-start(f32[2,256]{1,0:T(2,128)} %get-tuple-element.74) | copy-start | bytes 6148
  1623.7 86.0 %copy-start.4 = (f32[2304]{0:T(1024)S(1)}, f32[2304]{0:T(1024)}, u32[]{:S(2)}) copy-start(f32[2304]{0:T(1024)} %reshape.124) | copy-start | bytes 27652
  1623.7 86.0 %copy-start.5 = (f32[2304]{0:T(1024)S(1)}, f32[2304]{0:T(1024)}, u32[]{:S(2)}) copy-start(f32[2304]{0:T(1024)} %reshape.123) | copy-start | bytes 27652
  1623.7 86.0 %copy-start.16 = (f32[14]{0:T(128)S(1)}, f32[14]{0:T(128)}, u32[]{:S(2)}) copy-start(f32[14]{0:T(128)} %reshape.126) | copy-start | bytes 172
  1623.7 86.0 %copy-start.17 = (f32[14]{0:T(128)S(1)}, f32[14]{0:T(128)}, u32[]{:S(2)}) copy-start(f32[14]{0:T(128)} %reshape.125) | copy-start | bytes 172
Sparse Core Ops, SparseCore 0:
  9.8 125.0 all-gather.3
  136.7 152.9 all-gather.5
  946.4 279.3 reduce-scatter.4
  1229.9 369.9 reduce-scatter.2
